TPU v7x, 256 devices: a 4x2x16 block of a 4x16x16 slice. The times are simulated.
256 devices in a mesh: parts: 2 (over y), row: 16 (over z), chan: 4 (over x), sub: 2 (over core).
Axes of the slice: x: 4, y: 2, z: 16, core: 2. Of those that a mesh axis runs over, the one named last changes fastest.
The devices are a block of a 4x16x16 slice.
Arguments:
- pair: bfloat16 [896, 448, 128], P(('parts', 'row', 'sub'), 'chan'), parts along dimension 0, may hold values from -6 to 6
- pair_mask: int32 [896, 448], P(('parts', 'row', 'sub'), 'chan'), parts along dimension 0, may hold values 0 or 1
- out_in_gain: float32 [128], replicated, may hold values from 0.5 to 1.5
- out_proj: bfloat16 [128, 640], replicated, may hold values from -0.5 to 0.5
- out_mid_gain: float32 [128], replicated, may hold values from 0.5 to 1.5
- out_final: bfloat16 [128, 128], replicated, may hold values from -0.5 to 0.5
- in_in_gain: float32 [128], replicated, may hold values from 0.5 to 1.5
- in_proj: bfloat16 [128, 640], replicated, may hold values from -0.5 to 0.5
- in_mid_gain: float32 [128], replicated, may hold values from 0.5 to 1.5
- in_final: bfloat16 [128, 128], replicated, may hold values from -0.5 to 0.5
Outputs:
- updated: bfloat16 [896, 448, 128], P(('parts', 'row', 'sub'), 'chan'), parts along dimension 0
There are 2 independent parts, one for each index of `parts`. A program takes and returns all parts, laid end to end along the dimension named above; an argument that names none is the same for every part. Nothing has to cross between parts.
All inputs are finite; a program needn't handle non-finite values. No bound on the sum of `pair_mask` on one device may be relied on, other than what follows from the above.
Results may differ from a plain program's by a relative error of at most 0.014.
Values may be sent and summed in bfloat16 or wider, within the bound.
No kernel may reach another device: no remote copies, remote signals or barrier semaphores. Data moves between devices by JAX's collectives and lax.ppermute only.
A program may use at most 64 MiB of HBM per device.

v0:
```python
import jax
import jax.numpy as jnp
from jax import lax
from jax.sharding import PartitionSpec as P


def norm_last(values, gain):
    mean = jnp.mean(values, axis=-1, keepdims=True)
    var = jnp.mean((values - mean) ** 2, axis=-1, keepdims=True)
    return (values - mean) / jnp.sqrt(var + 1e-05) * gain


def norm_first(values, gain):
    mean = jnp.mean(values, axis=0, keepdims=True)
    var = jnp.mean((values - mean) ** 2, axis=0, keepdims=True)
    return (values - mean) / jnp.sqrt(var + 1e-05) * gain[:, None, None]


def project(pair, pair_mask, in_gain, proj, left_form, right_form, left_across):
    hidden = (proj.shape[1] - pair.shape[2]) // 4
    normed = norm_last(pair.astype(jnp.float32), in_gain).astype(jnp.bfloat16)
    keep = pair_mask.astype(jnp.float32)
    left_raw = jnp.einsum(
        left_form, normed, proj[:, : 2 * hidden], preferred_element_type=jnp.float32
    )
    right_raw = jnp.einsum(
        right_form, normed, proj[:, 2 * hidden : 4 * hidden], preferred_element_type=jnp.float32
    )
    left_keep = keep.T[None] if left_across else keep[None]
    left = (jax.nn.sigmoid(left_raw[:hidden]) * left_raw[hidden:] * left_keep).astype(jnp.bfloat16)
    right = (jax.nn.sigmoid(right_raw[:hidden]) * right_raw[hidden:] * keep[None]).astype(
        jnp.bfloat16
    )
    gate = jax.nn.sigmoid(
        jnp.dot(normed, proj[:, 4 * hidden :], preferred_element_type=jnp.float32)
    )
    return (left, right, gate)


def finish(pair, product, gate, mid_gain, final):
    whole = lax.all_to_all(
        product.astype(jnp.bfloat16), "chan", split_axis=2, concat_axis=0, tiled=True
    ).astype(product.dtype)
    normed = norm_first(whole, mid_gain).astype(jnp.bfloat16)
    update = jnp.einsum("crq,cd->rqd", normed, final, preferred_element_type=jnp.float32)
    return (pair.astype(jnp.float32) + gate * update).astype(jnp.bfloat16)


def shards(
    pair,
    pair_mask,
    out_in_gain,
    out_proj,
    out_mid_gain,
    out_final,
    in_in_gain,
    in_proj,
    in_mid_gain,
    in_final,
):
    left, right, gate = project(
        pair, pair_mask, out_in_gain, out_proj, "rqd,de->erq", "rqd,de->erq", False
    )
    left, right = (
        lax.all_to_all(left, "chan", split_axis=0, concat_axis=2, tiled=True),
        lax.all_to_all(right, "chan", split_axis=0, concat_axis=2, tiled=True),
    )
    product = jnp.einsum(
        "cik,cjk->cij",
        left,
        lax.all_gather(right, ("row", "sub"), axis=1, tiled=True),
        preferred_element_type=jnp.float32,
    )
    middle = finish(pair, product, gate, out_mid_gain, out_final)
    left_in, right_in, gate_in = project(
        middle, pair_mask, in_in_gain, in_proj, "rqd,de->eqr", "rqd,de->erq", True
    )
    columns = lax.all_to_all(
        lax.all_to_all(left_in, "chan", split_axis=0, concat_axis=1, tiled=True),
        ("row", "sub"),
        split_axis=1,
        concat_axis=2,
        tiled=True,
    )
    right_in = lax.all_to_all(right_in, "chan", split_axis=0, concat_axis=2, tiled=True)
    product_in = jnp.einsum(
        "cik,ckj->cij",
        columns,
        lax.all_gather(right_in, ("row", "sub"), axis=1, tiled=True),
        preferred_element_type=jnp.float32,
    )
    return finish(middle, product_in, gate_in, in_mid_gain, in_final)


def solution(mesh):
    placed = (
        P(("parts", "row", "sub"), "chan", None),
        P(("parts", "row", "sub"), "chan"),
        P(),
        P(),
        P(),
        P(),
        P(),
        P(),
        P(),
        P(),
    )
    return jax.shard_map(
        shards,
        mesh=mesh,
        in_specs=placed,
        out_specs=P(("parts", "row", "sub"), "chan", None),
        check_vma=False,
    )
```

profile of v0, /device:TPU:33, one launch (start us, length us, event | category | flops | bytes accessed | tf_op | source)
XLA Modules:
  0.0 357.3 jit_solution(9563343300795367324)
XLA Ops:
  9.4 1.7 convolution_bitcast_fusion.2
  13.5 11.9 %all_to_all.108 = bf16[128,14,112]{2,1,0:T(8,128)(2,1)S(1)} all-to-all(bf16[128,14,112]{2,1,0:T(8,128)(2,1)S(1)} %copy.93), channel_id=1, replica_groups=mesh['parts'=2,'row'=16,'chan'=4,'sub'=2] {'chan'}, dimensions={0} | all-to-all | bytes 802816 | tf_op jit(solution)/shard_map/all_to_all | solution.py:66
  27.3 9.4 %all_to_all.109 = bf16[128,14,112]{2,1,0:T(8,128)(2,1)S(1)} all-to-all(bf16[128,14,112]{2,1,0:T(8,128)(2,1)S(1)} %copy.90), channel_id=1, replica_groups=mesh['parts'=2,'row'=16,'chan'=4,'sub'=2] {'chan'}, dimensions={0} | all-to-all | bytes 802816 | tf_op jit(solution)/shard_map/all_to_all | solution.py:65
  37.5 98.7 %all-gather.3.cloned.1.call-done = bf16[32,448,448]{2,0,1:T(8,128)(2,1)} async-done(((bf16[32,14,448]{2,0,1:T(8,128)(2,1)}), bf16[32,448,448]{2,0,1:T(8,128)(2,1)}) %all-gather.3.cloned.1.call-update) | async-done | bytes 12845072 | tf_op jit(solution)/shard_map/all_gather | solution.py:71
  136.2 26.0 %fusion.12 = bf16[32,14,448]{2,1,0:T(8,128)(2,1)S(1)} fusion(bf16[32,14,448]{2,1,0:T(8,128)(2,1)S(1)} %reshape.80, bf16[32,448,448]{2,0,1:T(8,128)(2,1)} %all-gather.3.cloned.1.call-done), kind=kOutput, calls=%fused_computation.20 | convolution fusion | flops 180031488 | bytes 13647872 | tf_op jit(solution)/shard_map/cik,cjk->cij/dot_general | solution.py:68
  162.2 2.0 copy.98
  164.2 2.1 reshape.82
  166.4 4.0 %all-to-all-start.2 = ((bf16[4,2,25088]{2,1,0:T(2,128)(2,1)}), bf16[4,2,25088]{2,1,0:T(2,128)(2,1)S(1)}, u32[]{:S(2)}, u32[]{:S(2)}) async-start(bf16[4,2,25088]{2,1,0:T(2,128)(2,1)} %reshape.82), calls=%async_computation.2 | async-start | bytes 802816 | tf_op jit(solution)/shard_map/all_to_all | solution.py:41
  171.8 6.3 %all-to-all-done.2 = bf16[4,2,25088]{2,1,0:T(2,128)(2,1)S(1)} async-done(((bf16[4,2,25088]{2,1,0:T(2,128)(2,1)}), bf16[4,2,25088]{2,1,0:T(2,128)(2,1)S(1)}, u32[]{:S(2)}, u32[]{:S(2)}) %all-to-all-start.2) | async-done | bytes 401440 | tf_op jit(solution)/shard_map/all_to_all | solution.py:41
  179.5 1.6 copy.99
  185.4 10.3 %all_to_all.110 = bf16[128,14,112]{2,1,0:T(8,128)(2,1)S(1)} all-to-all(bf16[128,14,112]{2,1,0:T(8,128)(2,1)S(1)} %copy.108), channel_id=1, replica_groups=mesh['parts'=2,'row'=16,'chan'=4,'sub'=2] {'chan'}, dimensions={0} | all-to-all | bytes 802816 | tf_op jit(solution)/shard_map/all_to_all | solution.py:85
  198.3 9.4 %all_to_all.111 = bf16[128,112,14]{1,2,0:T(8,128)(2,1)S(1)} all-to-all(bf16[128,112,14]{1,2,0:T(8,128)(2,1)S(1)} %copy.102), channel_id=1, replica_groups=mesh['parts'=2,'row'=16,'chan'=4,'sub'=2] {'chan'}, dimensions={0} | all-to-all | bytes 802816 | tf_op jit(solution)/shard_map/all_to_all | solution.py:79
  207.6 1.6 copy.123
  210.7 45.8 %all_to_all.112 = bf16[32,2,3136]{2,1,0:T(2,128)(2,1)S(1)} all-to-all(bf16[32,2,3136]{2,1,0:T(2,128)(2,1)S(1)} %reshape.84), channel_id=1, replica_groups=mesh['parts'=2,'row'=16,'chan'=4,'sub'=2] {'row','sub'}, dimensions={0} | all-to-all | bytes 802816 | tf_op jit(solution)/shard_map/all_to_all | solution.py:78
  256.5 1.7 reshape.85
  258.2 4.7 %copy.126 = bf16[32,14,32,14]{3,2,1,0:T(8,128)(2,1)} copy(bf16[32,14,32,14]{0,3,1,2:T(8,128)(2,1)S(1)} %bitcast.105) | data formatting | bytes 802816 | tf_op jit(solution)/shard_map/all_to_all | solution.py:78
  262.9 7.3 %reshape.81 = bf16[32,14,448]{2,1,0:T(8,128)(2,1)S(1)} reshape(bf16[32,14,32,14]{3,2,1,0:T(8,128)(2,1)} %copy.126) | data formatting | bytes 802816 | tf_op jit(solution)/shard_map/all_to_all | solution.py:78
  270.2 37.5 %all-gather.5.cloned.1.call-done = bf16[32,448,448]{2,0,1:T(8,128)(2,1)} async-done(((bf16[32,14,448]{2,0,1:T(8,128)(2,1)}), bf16[32,448,448]{2,0,1:T(8,128)(2,1)}) %all-gather.5.cloned.1.call-update) | async-done | bytes 12845072 | tf_op jit(solution)/shard_map/all_gather | solution.py:89
  307.7 20.7 %fusion.15 = bf16[32,14,448]{2,1,0:T(8,128)(2,1)S(1)} fusion(bf16[32,14,448]{2,1,0:T(8,128)(2,1)S(1)} %reshape.81, bf16[32,448,448]{2,0,1:T(8,128)(2,1)} %all-gather.5.cloned.1.call-done), kind=kOutput, calls=%fused_computation.21 | convolution fusion | flops 180031488 | bytes 13647872 | tf_op jit(solution)/shard_map/cik,ckj->cij/dot_general | solution.py:86
  330.0 2.1 reshape.86
  332.1 4.0 %all-to-all-start.6 = ((bf16[4,2,25088]{2,1,0:T(2,128)(2,1)}), bf16[4,2,25088]{2,1,0:T(2,128)(2,1)S(1)}, u32[]{:S(2)}, u32[]{:S(2)}) async-start(bf16[4,2,25088]{2,1,0:T(2,128)(2,1)} %reshape.86), calls=%async_computation.6 | async-start | bytes 802816 | tf_op jit(solution)/shard_map/all_to_all | solution.py:41
  336.1 2.0 fusion.7
  338.1 5.7 %all-to-all-done.6 = bf16[4,2,25088]{2,1,0:T(2,128)(2,1)S(1)} async-done(((bf16[4,2,25088]{2,1,0:T(2,128)(2,1)}), bf16[4,2,25088]{2,1,0:T(2,128)(2,1)S(1)}, u32[]{:S(2)}, u32[]{:S(2)}) %all-to-all-start.6) | async-done | bytes 401440 | tf_op jit(solution)/shard_map/all_to_all | solution.py:41
  345.2 1.6 copy.114
  (82 shorter events, 25.0 us)
Async XLA Ops:
  6.5 176.1 %copy-start = (bf16[128,128]{1,0:T(8,128)(2,1)S(1)}, bf16[128,128]{1,0:T(8,128)(2,1)}, u32[]{:S(2)}) copy-start(bf16[128,128]{1,0:T(8,128)(2,1)} %param.15) | copy-start | bytes 98308
  6.6 129.7 %all-gather.3.cloned.1.call-start = ((), (), s32[]{:S(2)}) async-start(), calls=%async_computation.7 | async-start | bytes 15138816 | tf_op jit(solution)/shard_map/all_gather | solution.py:71
  9.3 1.7 copy-start.2
  9.3 1.7 copy-start.14
  9.4 3.2 copy-start.9
  11.1 1.5 copy-start.8
  164.2 6.2 %copy-start.10 = (f32[14,112]{1,0:T(8,128)S(1)}, f32[14,112]{1,0:T(8,128)}, u32[]{:S(2)}) copy-start(f32[14,112]{1,0:T(8,128)} %copy-done.9) | copy-start | bytes 18820
  164.2 6.1 %copy-start.15 = (f32[128]{0:T(128)S(1)}, f32[128]{0:T(128)}, u32[]{:S(2)}) copy-start(f32[128]{0:T(128)} %param.12) | copy-start | bytes 1540
  166.4 11.7 %all-to-all-start.2 = ((bf16[4,2,25088]{2,1,0:T(2,128)(2,1)}), bf16[4,2,25088]{2,1,0:T(2,128)(2,1)S(1)}, u32[]{:S(2)}, u32[]{:S(2)}) async-start(bf16[4,2,25088]{2,1,0:T(2,128)(2,1)} %reshape.82), calls=%async_computation.2 | async-start | bytes 802816 | tf_op jit(solution)/shard_map/all_to_all | solution.py:41
  170.4 137.3 %all-gather.5.cloned.1.call-start = ((), (), s32[]{:S(2)}) async-start(), calls=%async_computation.8 | async-start | bytes 15138816 | tf_op jit(solution)/shard_map/all_gather | solution.py:89
  181.8 0.7 copy-start.11
  182.6 1.1 copy-start.13
  182.6 1.6 copy-start.6
  184.3 12.9 %copy-start.3 = (bf16[14,112,128]{2,1,0:T(8,128)(2,1)}, bf16[14,112,128]{2,1,0:T(8,128)(2,1)S(1)}, u32[]{:S(2)}) copy-start(bf16[14,112,128]{2,1,0:T(8,128)(2,1)S(1)} %multiply_convert_fusion) | copy-start | bytes 1204228
  329.9 6.1 %copy-start.4 = (bf16[14,112,128]{2,1,0:T(8,128)(2,1)S(1)}, bf16[14,112,128]{2,1,0:T(8,128)(2,1)}, u32[]{:S(2)}) copy-start(bf16[14,112,128]{2,1,0:T(8,128)(2,1)} %copy-done.3) | copy-start | bytes 1204228
  332.1 11.7 %all-to-all-start.6 = ((bf16[4,2,25088]{2,1,0:T(2,128)(2,1)}), bf16[4,2,25088]{2,1,0:T(2,128)(2,1)S(1)}, u32[]{:S(2)}, u32[]{:S(2)}) async-start(bf16[4,2,25088]{2,1,0:T(2,128)(2,1)} %reshape.86), calls=%async_computation.6 | async-start | bytes 802816 | tf_op jit(solution)/shard_map/all_to_all | solution.py:41
  347.5 0.7 copy-start.12
  348.0 1.1 copy-start.5
  348.0 1.1 copy-start.7
  348.0 2.2 copy-start.1
Sparse Core Ops, SparseCore 0:
  27.0 109.2 all-gather.2
  197.3 110.3 all-gather.4
where the time goes:
time: 362 us; the launch traced here: 357 us
  waiting for transfers between devices  148 us (41%)
  blocking collectives  86.7 us (24%)
  matrix products  55.5 us (15%)
  local copies, waits for them, and re-layouts  38.5 us (11%)
  between operations  14.2 us (4%)
  starting transfers between devices  7.98 us (2%)
  other arithmetic  6.1 us (2%)
    all_gather x1, waiting for transfers between devices, shards(): lax.all_gather(right, ('row', 'sub'), axis=1, tiled=True)  98.7 us
    all_to_all x1, blocking collectives, shards(): lax.all_to_all(lax.all_to_all(left_in, 'chan', split_axis=0, concat_axis=...  45.8 us
    all_gather x1, waiting for transfers between devices, shards(): lax.all_gather(right_in, ('row', 'sub'), axis=1, tiled=True)  37.5 us
    dot_general x1, matrix products, shards(): jnp.einsum('cik,cjk->cij', left, lax.all_gather(right, ('row', 'sub'), ax...  26 us
    dot_general x1, matrix products, shards(): jnp.einsum('cik,ckj->cij', columns, lax.all_gather(right_in, ('row', 'sub...  20.7 us
    all_to_all x2, local copies, waits for them, and re-layouts, shards(): lax.all_to_all(lax.all_to_all(left_in, 'chan', split_axis=0, concat_axis=...  12 us
    all_to_all x2, waiting for transfers between devices, finish(): lax.all_to_all(product.astype(jnp.bfloat16), 'chan', split_axis=2, concat...  12 us
    all_to_all x1, blocking collectives, shards(): lax.all_to_all(right, 'chan', split_axis=0, concat_axis=2, tiled=True)  11.9 us
  transfers between devices with their start and end apart: 4, of which 4 were waited for; matrix products, arithmetic and copies ran while one was open for 6% of the time, Pallas kernels for 0%

commit v1 on v0

--- a/solution.py
+++ b/solution.py
@@ -1,7 +1,22 @@
+import functools
 import jax
 import jax.numpy as jnp
 from jax import lax
 from jax.sharding import PartitionSpec as P
+
+
+def keep_up_the_sections(local_array, ax_name):
+    nd = lax.axis_size(ax_name)
+    return lax.all_to_all(
+        jnp.tile(local_array, [nd if ii == 1 else 1 for ii in range(local_array.ndim)]),
+        ax_name,
+        split_axis=1,
+        concat_axis=1,
+        tiled=True,
+    )
+
+
+name_the_modes = functools.partial(keep_up_the_sections, ax_name=("row", "sub"))
 
 
 def norm_last(values, gain):
@@ -84,10 +99,7 @@
     )
     right_in = lax.all_to_all(right_in, "chan", split_axis=0, concat_axis=2, tiled=True)
     product_in = jnp.einsum(
-        "cik,ckj->cij",
-        columns,
-        lax.all_gather(right_in, ("row", "sub"), axis=1, tiled=True),
-        preferred_element_type=jnp.float32,
+        "cik,ckj->cij", columns, name_the_modes(right_in), preferred_element_type=jnp.float32
     )
     return finish(middle, product_in, gate_in, in_mid_gain, in_final)
 

time: 362 us -> 953 us (2.63); the launches traced: 357 us -> 936 us
  waiting for transfers between devices: 148 us -> 755 us
  blocking collectives: 86.7 us -> 21.2 us
  starting transfers between devices: 7.98 us -> 33.4 us
  local copies, waits for them, and re-layouts: 38.5 us -> 50.1 us
    all_to_all x0 -> x4, waiting for transfers between devices: none -> 645 us  [the longest x1 609 us: keep_up_the_sections(): lax.all_to_all(jnp.tile(local_array, [nd if ii == 1 else 1 for ii in rang...]
    all_to_all x3 -> x0, blocking collectives: 65.5 us -> none  [the longest x1 45.8 us: shards(): lax.all_to_all(lax.all_to_all(left_in, 'chan', split_axis=0, concat_axis=...]
    all_gather x1 -> x0, waiting for transfers between devices: 37.5 us -> none  [shards(): lax.all_gather(right_in, ('row', 'sub'), axis=1, tiled=True)]
    all_to_all x0 -> x4, starting transfers between devices: none -> 25.8 us  [the longest x1 12.9 us: shards(): lax.all_to_all(lax.all_to_all(left_in, 'chan', split_axis=0, concat_axis=...]
  transfers between devices with their start and end apart: 4 -> 7, of which waited for: 4 -> 7; matrix products, arithmetic and copies ran while one was open for 6% -> 3% of each run, Pallas kernels for 0% -> 0%
where the time goes in v1:
time: 953 us; the launch traced here: 936 us
  waiting for transfers between devices  755 us (79%)
  matrix products  55.6 us (6%)
  local copies, waits for them, and re-layouts  50.1 us (5%)
  starting transfers between devices  33.4 us (4%)
  blocking collectives  21.2 us (2%)
  between operations  14.2 us (1%)
    all_to_all x1, waiting for transfers between devices, keep_up_the_sections(): lax.all_to_all(jnp.tile(local_array, [nd if ii == 1 else 1 for ii in rang...  609 us
    all_gather x1, waiting for transfers between devices, shards(): lax.all_gather(right, ('row', 'sub'), axis=1, tiled=True)  98.7 us
    all_to_all x1, waiting for transfers between devices, shards(): lax.all_to_all(lax.all_to_all(left_in, 'chan', split_axis=0, concat_axis=...  27.5 us
    dot_general x1, matrix products, shards(): jnp.einsum('cik,cjk->cij', left, lax.all_gather(right, ('row', 'sub'), ax...  26.8 us
    dot_general x1, matrix products, shards(): jnp.einsum('cik,ckj->cij', columns, name_the_modes(right_in), preferred_e...  20.7 us
  transfers between devices with their start and end apart: 7, of which 7 were waited for; matrix products, arithmetic and copies ran while one was open for 3% of the time, Pallas kernels for 0%

profile of v1, /device:TPU:33, one launch (start us, length us, event | category | flops | bytes accessed | tf_op | source)
XLA Modules:
  0.0 935.8 jit_solution(14139698481598518937)
XLA Ops:
  12.7 11.9 %all_to_all.110 = bf16[128,14,112]{2,1,0:T(8,128)(2,1)S(1)} all-to-all(bf16[128,14,112]{2,1,0:T(8,128)(2,1)S(1)} %copy.92), channel_id=1, replica_groups=mesh['parts'=2,'row'=16,'chan'=4,'sub'=2] {'chan'}, dimensions={0} | all-to-all | bytes 802816 | tf_op jit(solution)/shard_map/all_to_all | solution.py:81
  26.5 9.4 %all_to_all.111 = bf16[128,14,112]{2,1,0:T(8,128)(2,1)S(1)} all-to-all(bf16[128,14,112]{2,1,0:T(8,128)(2,1)S(1)} %copy.89), channel_id=1, replica_groups=mesh['parts'=2,'row'=16,'chan'=4,'sub'=2] {'chan'}, dimensions={0} | all-to-all | bytes 802816 | tf_op jit(solution)/shard_map/all_to_all | solution.py:80
  36.7 98.7 %all-gather.2.cloned.1.call-done = bf16[32,448,448]{2,0,1:T(8,128)(2,1)} async-done(((bf16[32,14,448]{2,0,1:T(8,128)(2,1)}), bf16[32,448,448]{2,0,1:T(8,128)(2,1)}) %all-gather.2.cloned.1.call-update) | async-done | bytes 12845072 | tf_op jit(solution)/shard_map/all_gather | solution.py:86
  135.4 26.8 %fusion.12 = bf16[32,14,448]{2,1,0:T(8,128)(2,1)} fusion(bf16[32,14,448]{2,1,0:T(8,128)(2,1)S(1)} %reshape.85, bf16[32,448,448]{2,0,1:T(8,128)(2,1)} %all-gather.2.cloned.1.call-done), kind=kOutput, calls=%fused_computation.20 | convolution fusion | flops 180031488 | bytes 13647872 | tf_op jit(solution)/shard_map/cik,cjk->cij/dot_general | solution.py:83
  162.2 3.1 copy.97
  165.3 2.1 reshape.87
  167.5 4.0 all-to-all-start.2
  173.0 6.2 all-to-all-done.2
  187.9 3.6 all-to-all-start.3
  193.4 5.9 all-to-all-done.3
  199.3 3.6 all-to-all-start.5
  202.9 2.7 copy.122
  205.6 2.1 reshape.89
  209.7 12.9 %all-to-all-start.4 = ((bf16[32,2,3136]{2,1,0:T(2,128)(2,1)}), bf16[32,2,3136]{2,1,0:T(2,128)(2,1)S(1)}, u32[]{:S(2)}, u32[]{:S(2)}) async-start(bf16[32,2,3136]{2,1,0:T(2,128)(2,1)} %reshape.89), calls=%async_computation.4 | async-start | bytes 819200 | tf_op jit(solution)/shard_map/all_to_all | solution.py:93
  223.3 27.5 %all-to-all-done.4 = bf16[32,2,3136]{2,1,0:T(2,128)(2,1)S(1)} async-done(((bf16[32,2,3136]{2,1,0:T(2,128)(2,1)}), bf16[32,2,3136]{2,1,0:T(2,128)(2,1)S(1)}, u32[]{:S(2)}, u32[]{:S(2)}) %all-to-all-start.4) | async-done | bytes 401440 | tf_op jit(solution)/shard_map/all_to_all | solution.py:93
  250.8 7.0 tile.12
  257.8 5.8 all-to-all-start.6
  265.3 4.7 copy.125
  270.1 7.3 reshape.86
  277.4 609.3 %all-to-all-done.6 = bf16[32,448,448]{2,0,1:T(8,128)(2,1)} async-done(((bf16[32,448,448]{2,0,1:T(8,128)(2,1)}), bf16[32,448,448]{2,0,1:T(8,128)(2,1)}, u32[]{:S(2)}, u32[]{:S(2)}) %all-to-all-start.6) | async-done | bytes 12845088 | tf_op jit(solution)/shard_map/all_to_all | solution.py:10
  886.7 20.7 %fusion.15 = bf16[32,14,448]{2,1,0:T(8,128)(2,1)S(1)} fusion(bf16[32,14,448]{2,1,0:T(8,128)(2,1)S(1)} %reshape.86, bf16[32,448,448]{2,0,1:T(8,128)(2,1)} %all-to-all-done.6), kind=kOutput, calls=%fused_computation.21 | convolution fusion | flops 180031488 | bytes 13647872 | tf_op jit(solution)/shard_map/cik,ckj->cij/dot_general | solution.py:101
  908.9 2.1 reshape.91
  911.1 3.6 all-to-all-start.7
  916.7 5.6 all-to-all-done.7
  (89 shorter events, 35.0 us)
Async XLA Ops:
  6.5 177.1 %copy-start = (bf16[128,128]{1,0:T(8,128)(2,1)S(1)}, bf16[128,128]{1,0:T(8,128)(2,1)}, u32[]{:S(2)}) copy-start(bf16[128,128]{1,0:T(8,128)(2,1)} %param.15) | copy-start | bytes 98308
  6.6 128.9 %all-gather.2.cloned.1.call-start = ((), (), s32[]{:S(2)}) async-start(), calls=%async_computation.8 | async-start | bytes 15138816 | tf_op jit(solution)/shard_map/all_gather | solution.py:86
  9.3 1.7 copy-start.2
  9.3 1.7 copy-start.16
  9.4 1.7 copy-start.17
  11.1 0.7 copy-start.12
  167.5 11.7 %all-to-all-start.2 = ((bf16[4,2,25088]{2,1,0:T(2,128)(2,1)}), bf16[4,2,25088]{2,1,0:T(2,128)(2,1)S(1)}, u32[]{:S(2)}, u32[]{:S(2)}) async-start(bf16[4,2,25088]{2,1,0:T(2,128)(2,1)} %reshape.87), calls=%async_computation.2 | async-start | bytes 802816 | tf_op jit(solution)/shard_map/all_to_all | solution.py:56
  182.8 0.7 copy-start.13
  183.3 1.1 copy-start.8
  184.5 1.1 copy-start.15
  184.5 1.6 copy-start.10
  186.1 5.4 copy-start.3
  187.9 11.3 %all-to-all-start.3 = ((bf16[128,112,14]{1,2,0:T(8,128)(2,1)}), bf16[128,112,14]{1,2,0:T(8,128)(2,1)S(1)}, u32[]{:S(2)}, u32[]{:S(2)}) async-start(bf16[128,112,14]{1,2,0:T(8,128)(2,1)} %copy.101), calls=%async_computation.3 | async-start | bytes 1048576 | tf_op jit(solution)/shard_map/all_to_all | solution.py:94
  199.3 3.6 copy-start.5
  199.3 10.4 %all-to-all-start.5 = ((bf16[128,14,112]{2,1,0:T(8,128)(2,1)}), bf16[128,14,112]{2,1,0:T(8,128)(2,1)S(1)}, u32[]{:S(2)}, u32[]{:S(2)}) async-start(bf16[128,14,112]{2,1,0:T(8,128)(2,1)} %copy.107), calls=%async_computation.5 | async-start | bytes 1048576 | tf_op jit(solution)/shard_map/all_to_all | solution.py:100
  209.7 41.1 %all-to-all-start.4 = ((bf16[32,2,3136]{2,1,0:T(2,128)(2,1)}), bf16[32,2,3136]{2,1,0:T(2,128)(2,1)S(1)}, u32[]{:S(2)}, u32[]{:S(2)}) async-start(bf16[32,2,3136]{2,1,0:T(2,128)(2,1)} %reshape.89), calls=%async_computation.4 | async-start | bytes 819200 | tf_op jit(solution)/shard_map/all_to_all | solution.py:93
  250.8 7.0 copy-start.6
  257.8 5.8 copy-start.7
  257.8 628.8 %all-to-all-start.6 = ((bf16[32,448,448]{2,0,1:T(8,128)(2,1)}), bf16[32,448,448]{2,0,1:T(8,128)(2,1)}, u32[]{:S(2)}, u32[]{:S(2)}) async-start(bf16[32,448,448]{2,0,1:T(8,128)(2,1)} %bitcast.99), calls=%async_computation.6 | async-start | bytes 29360128 | tf_op jit(solution)/shard_map/all_to_all | solution.py:10
  908.9 5.7 copy-start.4
  911.1 11.2 %all-to-all-start.7 = ((bf16[4,2,25088]{2,1,0:T(2,128)(2,1)}), bf16[4,2,25088]{2,1,0:T(2,128)(2,1)S(1)}, u32[]{:S(2)}, u32[]{:S(2)}) async-start(bf16[4,2,25088]{2,1,0:T(2,128)(2,1)} %reshape.91), calls=%async_computation.7 | async-start | bytes 802816 | tf_op jit(solution)/shard_map/all_to_all | solution.py:56
  926.5 1.1 copy-start.9
  926.5 1.1 copy-start.11
  926.5 2.2 copy-start.1
  (1 other events, 0.7 us)
Sparse Core Ops, SparseCore 0:
  26.2 109.2 all-gather.1
